TPU v7x, 32 devices: a whole 2x2x4 slice. The times are simulated.
32 devices in a mesh: grp: 8 (over z, y), rep: 4 (over x, core).
Axes of the slice: x: 2, y: 2, z: 4, core: 2. Of those that a mesh axis runs over, the one named last changes fastest.
Arguments:
- queries: bfloat16 [16, 4, 32, 128], P('grp', 'rep'), may hold values from -3.2 to 3.2
- passages: bfloat16 [512, 4, 180, 128], P('grp', 'rep'), may hold values from -1.796875 to 1.796875
- lengths: int32 [512, 4], P('grp', 'rep'), may hold values from 16 to 180
- cand_ids: int32 [16, 4, 64], P('grp', 'rep'), may hold values from 0 to 511, as said below
- owner_map: int32 [4, 512], P('rep'), may hold values from 0 to 511, as said below
- teacher: float32 [16, 4, 64], P('grp', 'rep'), may hold values from -12 to 312
- weights: float32 [16, 4], P('grp', 'rep'), may hold values from 0.5 to 18
Outputs:
- loss: float32 [], replicated
- query_grad: float32 [16, 4, 32, 128], P('grp', 'rep')
- passage_grad: bfloat16 [512, 4, 180, 128], P('grp', 'rep')
Inputs may be any that keep to these rules, and one draw needn't show every extreme that they name: `cand_ids`: within each replica, the 128 candidates of the queries of one grp index have storage rows of which at most 32 (counted with repeats) lie in any one aligned block of 64 rows; in every draw, in each replica, one block receives exactly 32 from every grp index. `owner_map`: each row is a permutation of 0 to 511.
All inputs are finite; a program needn't handle non-finite values.
Results may differ from a plain program's by a relative error of at most 0.0055.
Values may be sent and summed in bfloat16 or wider, within the bound.
A program may use at most 128 MiB of HBM per device.

v0:
```python
import jax
import jax.numpy as jnp
from jax import lax
from jax.sharding import PartitionSpec as P

temper = 0.05


def token_softmax(products, lengths_used):
    usable = (
        lax.broadcasted_iota(jnp.int32, products.shape, products.ndim - 1)
        < lengths_used[..., None, None]
    )
    scaled = jnp.where(usable, products / temper, -1e30)
    highest = jnp.max(scaled, axis=-1, keepdims=True)
    powers = jnp.where(usable, jnp.exp(scaled - highest), 0.0)
    summed = jnp.sum(powers, axis=-1, keepdims=True)
    matched = temper * (highest[..., 0] + jnp.log(summed[..., 0]))
    return (matched, powers / summed)


def on_device(queries, passages, lengths, cand_ids, owner_map, teacher, weights):
    groups = lax.axis_size("grp")
    replicas = lax.axis_size("rep")
    query_local = queries.shape[0]
    query_len = queries.shape[2]
    feature_dim = queries.shape[3]
    passage_local = passages.shape[0]
    token_len = passages.shape[2]
    candidates = cand_ids.shape[2]
    ref_count = query_local * candidates
    capacity = 2 * ref_count // groups
    slot_count = groups * capacity
    block_width = token_len * feature_dim
    query_width = query_len * feature_dim
    position_table = owner_map[0]
    wanted = cand_ids[:, 0, :].reshape(ref_count)
    table_index = jnp.arange(position_table.shape[0], dtype=jnp.int32)
    positions = jnp.sum(
        jnp.where(wanted[:, None] == table_index[None, :], position_table[None, :], 0), axis=1
    )
    owner_index = positions // passage_local
    local_row = positions % passage_local
    owner_hot = (owner_index[:, None] == jnp.arange(groups, dtype=jnp.int32)[None, :]).astype(
        jnp.int32
    )
    before = jnp.cumsum(owner_hot, axis=0) - owner_hot
    slot_rank = jnp.sum(before * owner_hot, axis=1)
    slot_index = owner_index * capacity + slot_rank
    request = jnp.full((slot_count,), -1, jnp.int32).at[slot_index].set(local_row)
    asked_rows = lax.all_to_all(
        request.reshape(groups, capacity), "grp", split_axis=0, concat_axis=0, tiled=True
    ).reshape(slot_count)
    present = asked_rows >= 0
    safe_rows = jnp.maximum(asked_rows, 0)
    slot_lengths = jnp.where(present, lengths[:, 0][safe_rows], 0)
    stored_index = jnp.arange(passage_local, dtype=jnp.int32)
    gather_hot = (asked_rows[None, :] == stored_index[:, None]).astype(jnp.bfloat16)
    pick_hot = (asked_rows[:, None] == stored_index[None, :]).astype(jnp.bfloat16)
    route_hot = (slot_index[:, None] == jnp.arange(slot_count, dtype=jnp.int32)[None, :]).astype(
        jnp.bfloat16
    )
    flat_passages = passages.reshape(passage_local, block_width)
    query_flat = queries[:, 0]
    query_weights = weights[:, 0]
    query_source = jnp.arange(ref_count, dtype=jnp.int32) // candidates
    blocks_flat = jnp.dot(pick_hot, flat_passages, preferred_element_type=jnp.float32).astype(
        jnp.bfloat16
    )
    ref_queries = query_flat[query_source].reshape(ref_count, query_width)
    slot_queries = jnp.einsum(
        "rs,rk->sk", route_hot, ref_queries, preferred_element_type=jnp.float32
    ).astype(jnp.bfloat16)
    got_queries = lax.all_to_all(
        slot_queries.reshape(groups, capacity, query_width),
        "grp",
        split_axis=0,
        concat_axis=0,
        tiled=True,
    )
    got_queries = got_queries.reshape(slot_count, query_len, feature_dim)
    blocks = blocks_flat.reshape(slot_count, token_len, feature_dim)
    products = jnp.einsum("sid,sjd->sij", got_queries, blocks, preferred_element_type=jnp.float32)
    matched, attention = token_softmax(products, jnp.maximum(slot_lengths, 1))
    slot_scores = jnp.sum(matched, axis=-1)
    back_scores = lax.all_to_all(
        slot_scores.reshape(groups, capacity), "grp", split_axis=0, concat_axis=0, tiled=True
    ).reshape(slot_count)
    student = back_scores[slot_index].reshape(query_local, candidates)
    log_student = jax.nn.log_softmax(student, axis=-1)
    log_teacher = jax.nn.log_softmax(teacher[:, 0], axis=-1)
    teacher_prob = jnp.exp(log_teacher)
    divergence = jnp.sum(teacher_prob * (log_teacher - log_student), axis=-1)
    totals = lax.psum((jnp.sum(query_weights * divergence), jnp.sum(query_weights)), ("grp", "rep"))
    loss_value = totals[0] / totals[1]
    scale_all = query_local * groups * replicas
    score_grad = (
        scale_all * query_weights[:, None] / totals[1] * (jnp.exp(log_student) - teacher_prob)
    )
    loss_value, score_grad = (loss_value, score_grad)
    slot_score_grad = (
        jnp.zeros((slot_count,), jnp.float32).at[slot_index].set(score_grad.reshape(ref_count))
    )
    arrived = lax.all_to_all(
        slot_score_grad.reshape(groups, capacity), "grp", split_axis=0, concat_axis=0, tiled=True
    ).reshape(slot_count)
    scaled_grad = (arrived[:, None, None] * attention).astype(jnp.bfloat16)
    pair_query = jnp.einsum(
        "sij,sjd->sid", scaled_grad, blocks, preferred_element_type=jnp.float32
    ).astype(jnp.bfloat16)
    returned_queries = lax.all_to_all(
        pair_query.reshape(groups, capacity, query_width),
        "grp",
        split_axis=0,
        concat_axis=0,
        tiled=True,
    )
    ordered = jnp.dot(
        route_hot,
        returned_queries.reshape(slot_count, query_width),
        preferred_element_type=jnp.float32,
    )
    query_grad = jnp.sum(ordered.reshape(query_local, candidates, query_len, feature_dim), axis=1)
    returned = jnp.einsum(
        "sij,sid->sjd", scaled_grad, got_queries, preferred_element_type=jnp.float32
    ).astype(jnp.bfloat16)
    returned = returned.reshape(slot_count, block_width)
    passage_sum = jnp.dot(gather_hot, returned, preferred_element_type=jnp.float32)
    passage_grad = passage_sum.astype(jnp.bfloat16).reshape(
        passage_local, 1, token_len, feature_dim
    )
    return (loss_value, query_grad[:, None], passage_grad)


def solution(mesh):
    return jax.shard_map(
        on_device,
        mesh=mesh,
        in_specs=(
            P("grp", "rep", None, None),
            P("grp", "rep", None, None),
            P("grp", "rep"),
            P("grp", "rep", None),
            P("rep", None),
            P("grp", "rep", None),
            P("grp", "rep"),
        ),
        out_specs=(P(), P("grp", "rep", None, None), P("grp", "rep", None, None)),
        check_vma=False,
    )
```

profile of v0, /device:TPU:0, one launch (start us, length us, event | category | flops | bytes accessed | tf_op | source)
XLA Modules:
  0.0 235.0 jit_solution(7812070350902260653)
XLA Ops:
  0.7 0.5 broadcast.316
  1.2 1.3 reduce.17
  2.6 0.9 select_reduce_fusion
  3.6 0.2 reduce_window_sum.11
  3.7 0.2 select_reduce_fusion.1
  3.9 1.0 scatter_custom_fusion
  4.9 0.7 all_to_all.24
  5.6 7.3 %all-to-all-start = ((s32[8,1,32]{2,1,0:T(1,128)}), s32[8,1,32]{2,1,0:T(1,128)S(1)}, u32[]{:S(2)}, u32[]{:S(2)}) async-start(s32[8,1,32]{2,1,0:T(1,128)} %all_to_all.24), calls=%async_computation | async-start | bytes 8192 | tf_op jit(solution)/shard_map/all_to_all | solution.py:51
  13.0 0.8 gather_fusion.1
  13.7 2.2 convolution_convert_fusion.3
  15.9 3.4 %all-to-all-done = s32[8,1,32]{2,1,0:T(1,128)S(1)} async-done(((s32[8,1,32]{2,1,0:T(1,128)}), s32[8,1,32]{2,1,0:T(1,128)S(1)}, u32[]{:S(2)}, u32[]{:S(2)}) %all-to-all-start) | async-done | bytes 1056 | tf_op jit(solution)/shard_map/all_to_all | solution.py:51
  19.3 4.4 %all-to-all-start.1 = ((bf16[8,32,4096]{2,1,0:T(8,128)(2,1)}), bf16[8,32,4096]{2,1,0:T(8,128)(2,1)}, u32[]{:S(2)}, u32[]{:S(2)}) async-start(bf16[8,32,4096]{2,1,0:T(8,128)(2,1)} %bitcast.9), calls=%async_computation.1 | async-start | bytes 4194304 | tf_op jit(solution)/shard_map/all_to_all | solution.py:74
  23.7 3.7 %copy.19 = bf16[64,1,180,128]{3,2,0,1:T(8,128)(2,1)S(1)} copy(bf16[64,1,180,128]{3,0,2,1:T(8,128)(2,1)} %param.9) | data formatting | bytes 5898240 | tf_op args[1]
  27.6 0.2 exponential_reduce_fusion.1
  27.8 0.7 maximum_reduce_fusion
  28.6 6.2 %convolution_convert_fusion = bf16[256,23040]{1,0:T(8,128)(2,1)} fusion(bf16[8,8,180,128]{3,2,1,0:T(8,128)(2,1)S(1)} %bitcast.67, s32[256]{0:T(256)S(1)} %reshape.239), kind=kOutput, calls=%fused_computation.5 | convolution fusion | flops 760889344 | bytes 14746624 | tf_op jit(solution)/shard_map/dot_general | solution.py:67
  34.8 16.2 %copy.20 = bf16[256,23040]{0,1:T(8,128)(2,1)} copy(bf16[256,23040]{1,0:T(8,128)(2,1)} %convolution_convert_fusion) | data formatting | bytes 23592960 | tf_op jit(solution)/shard_map/convert_element_type | solution.py:67
  51.0 16.5 %copy.21 = bf16[256,180,128]{2,1,0:T(8,128)(2,1)} copy(bf16[256,180,128]{0,2,1:T(8,128)(2,1)} %bitcast.66) | data formatting | bytes 23592960 | tf_op jit(solution)/shard_map/reshape | solution.py:82
  67.6 1.9 gather_fusion
  69.5 1.3 all-to-all-done.1
  70.8 2.1 copy.28
  72.9 15.2 %fusion = (f32[256,32]{1,0:T(8,128)S(1)}, f32[256,32,180]{2,1,0:T(8,128)}) fusion(s32[256]{0:T(256)S(1)} %fusion.13, bf16[256,32,128]{2,1,0:T(8,128)(2,1)S(1)} %bitcast.69, bf16[256,180,128]{2,1,0:T(8,128)(2,1)} %copy.21), kind=kOutput, calls=%fused_computation.12 | convolution fusion | flops 383377408 | bytes 19825664 | tf_op jit(solution)/shard_map/sid,sjd->sij/dot_general | solution.py:83
  88.1 6.4 %fusion.1 = f32[256,32]{1,0:T(8,128)S(1)} fusion(f32[256,32,180]{2,1,0:T(8,128)} %get-tuple-element.20, f32[256,32]{1,0:T(8,128)S(1)} %get-tuple-element.19, s32[256]{0:T(256)S(1)} %fusion.13), kind=kLoop, calls=%fused_computation.14 | loop fusion | flops 8839168 | bytes 5964800 | tf_op jit(solution)/shard_map/reduce_sum | solution.py:17
  94.7 0.7 all_to_all.27
  95.3 4.6 %all-to-all-start.2 = ((f32[8,1,32]{2,1,0:T(1,128)}), f32[8,1,32]{2,1,0:T(1,128)S(1)}, u32[]{:S(2)}, u32[]{:S(2)}) async-start(f32[8,1,32]{2,1,0:T(1,128)} %all_to_all.27), calls=%async_computation.2 | async-start | bytes 8192 | tf_op jit(solution)/shard_map/all_to_all | solution.py:86
  100.0 0.6 reduce_sum.97
  100.6 5.8 %all-to-all-done.2 = f32[8,1,32]{2,1,0:T(1,128)S(1)} async-done(((f32[8,1,32]{2,1,0:T(1,128)}), f32[8,1,32]{2,1,0:T(1,128)S(1)}, u32[]{:S(2)}, u32[]{:S(2)}) %all-to-all-start.2) | async-done | bytes 1056 | tf_op jit(solution)/shard_map/all_to_all | solution.py:86
  106.3 0.5 broadcast.318
  106.9 0.7 reduce.19
  107.6 1.3 gather_fusion.2
  109.1 0.2 exponential_reduce_fusion
  109.3 0.2 multiply_reduce_fusion.1
  109.5 0.6 fusion.16
  110.1 38.7 %all-reduce = (f32[]{:T(128)}, f32[]{:T(128)}) all-reduce(f32[]{:T(128)} %fusion.16, f32[]{:T(128)} %reduce_sum.97), channel_id=1, replica_groups=mesh['grp'=8,'rep'=4] {'grp','rep'}, use_global_device_ids=true, to_apply=%region_11.13 | all-reduce | flops 2 | bytes 16 | tf_op jit(solution)/shard_map/psum | solution.py:94
  148.8 0.7 divide_bitcast_fusion
  149.6 1.0 scatter_custom_fusion.1
  150.7 11.1 %all_to_all.37 = f32[8,1,32]{2,1,0:T(1,128)S(1)} all-to-all(f32[8,1,32]{2,1,0:T(1,128)S(1)} %all_to_all.29), channel_id=1, replica_groups=mesh['grp'=8,'rep'=4] {'grp'}, dimensions={0} | all-to-all | bytes 2048 | tf_op jit(solution)/shard_map/all_to_all | solution.py:104
  161.8 0.7 reduce.20
  162.5 10.3 %convolution_convert_fusion.4 = bf16[256,32,128]{2,1,0:T(8,128)(2,1)} fusion(bf16[256,180,128]{2,1,0:T(8,128)(2,1)} %copy.21, f32[256,32,180]{2,1,0:T(8,128)} %get-tuple-element.20, f32[256,32]{1,0:T(8,128)S(1)} %fusion.1, f32[256]{0:T(256)S(1)} %mul.78, f32[256,32]{1,0:T(8,128)S(1)} %get-tuple-element.19, s32[256]{0:T(256)S(1)} %fusion.13), kind=kOutput, calls=%fused_computation.17 | convolution fusion | flops 390332416 | bytes 19859456 | tf_op jit(solution)/shard_map/sij,sjd->sid/dot_general | solution.py:108
  172.8 4.2 %reshape.248 = bf16[8,32,4096]{2,1,0:T(8,128)(2,1)} reshape(bf16[256,32,128]{2,1,0:T(8,128)(2,1)} %convolution_convert_fusion.4) | data formatting | bytes 4194304 | tf_op jit(solution)/shard_map/reshape | solution.py:112
  177.0 4.4 %all-to-all-start.4 = ((bf16[8,32,4096]{2,1,0:T(8,128)(2,1)}), bf16[8,32,4096]{2,1,0:T(8,128)(2,1)}, u32[]{:S(2)}, u32[]{:S(2)}) async-start(bf16[8,32,4096]{2,1,0:T(8,128)(2,1)} %reshape.248), calls=%async_computation.4 | async-start | bytes 4194304 | tf_op jit(solution)/shard_map/all_to_all | solution.py:111
  182.9 14.7 %convolution_convert_fusion.2 = bf16[256,180,128]{2,1,0:T(8,128)(2,1)} fusion(bf16[256,32,128]{2,1,0:T(8,128)(2,1)S(1)} %bitcast.70, f32[256,32,180]{2,1,0:T(8,128)} %get-tuple-element.20, f32[256,32]{1,0:T(8,128)S(1)} %fusion.1, f32[256]{0:T(256)S(1)} %mul.78, f32[256,32]{1,0:T(8,128)S(1)} %get-tuple-element.19, s32[256]{0:T(256)S(1)} %fusion.13), kind=kOutput, calls=%fused_computation.11 | convolution fusion | flops 395182080 | bytes 19859456 | tf_op jit(solution)/shard_map/sij,sid->sjd/dot_general | solution.py:124
  197.6 16.4 %copy.24 = bf16[256,180,128]{0,2,1:T(8,128)(2,1)} copy(bf16[256,180,128]{2,1,0:T(8,128)(2,1)} %convolution_convert_fusion.2) | data formatting | bytes 23592960 | tf_op jit(solution)/shard_map/convert_element_type | solution.py:126
  214.0 8.0 %convolution_convert_fusion.1 = bf16[64,23040]{1,0:T(8,128)(2,1)S(1)} fusion(bf16[256,23040]{0,1:T(8,128)(2,1)} %bitcast.65, s32[256]{0:T(256)S(1)} %reshape.239), kind=kOutput, calls=%fused_computation.6 | convolution fusion | flops 756465664 | bytes 14746624 | tf_op jit(solution)/shard_map/dot_general | solution.py:128
  222.0 2.9 %reshape.251 = bf16[64,1,180,128]{3,2,0,1:T(8,128)(2,1)} reshape(bf16[64,23040]{1,0:T(8,128)(2,1)S(1)} %convolution_convert_fusion.1) | data formatting | bytes 5898240 | tf_op jit(solution)/shard_map/reshape | solution.py:129
  224.9 4.2 %copy.25 = bf16[64,1,180,128]{3,0,2,1:T(8,128)(2,1)} copy(bf16[64,1,180,128]{3,2,0,1:T(8,128)(2,1)} %reshape.251) | data formatting | bytes 5898240
  229.2 3.3 %copy.23 = bf16[256,4096]{0,1:T(8,128)(2,1)S(1)} copy(bf16[256,4096]{1,0:T(8,128)(2,1)} %bitcast.15) | data formatting | bytes 4194304 | tf_op jit(solution)/shard_map/reshape | solution.py:120
  232.4 1.4 convolution_reduce_fusion
  (37 shorter events, 1.5 us)
Async XLA Ops:
  0.6 12.3 %copy-start = (bf16[2,1,32,128]{3,2,1,0:T(8,128)(2,1)S(1)}, bf16[2,1,32,128]{3,2,1,0:T(8,128)(2,1)}, u32[]{:S(2)}) copy-start(bf16[2,1,32,128]{3,2,1,0:T(8,128)(2,1)} %param.8) | copy-start | bytes 49156
  0.6 26.8 %copy-start.3 = (f32[2,1,64]{2,1,0:T(1,128)S(1)}, f32[2,1,64]{2,1,0:T(1,128)}, u32[]{:S(2)}) copy-start(f32[2,1,64]{2,1,0:T(1,128)} %param.13) | copy-start | bytes 1540
  5.6 13.7 %all-to-all-start = ((s32[8,1,32]{2,1,0:T(1,128)}), s32[8,1,32]{2,1,0:T(1,128)S(1)}, u32[]{:S(2)}, u32[]{:S(2)}) async-start(s32[8,1,32]{2,1,0:T(1,128)} %all_to_all.24), calls=%async_computation | async-start | bytes 8192 | tf_op jit(solution)/shard_map/all_to_all | solution.py:51
  19.3 51.5 %all-to-all-start.1 = ((bf16[8,32,4096]{2,1,0:T(8,128)(2,1)}), bf16[8,32,4096]{2,1,0:T(8,128)(2,1)}, u32[]{:S(2)}, u32[]{:S(2)}) async-start(bf16[8,32,4096]{2,1,0:T(8,128)(2,1)} %bitcast.9), calls=%async_computation.1 | async-start | bytes 4194304 | tf_op jit(solution)/shard_map/all_to_all | solution.py:74
  51.0 16.5 %copy-start.2 = (s32[64,1]{0,1:T(1,128)S(1)}, s32[64,1]{0,1:T(1,128)}, u32[]{:S(2)}) copy-start(s32[64,1]{0,1:T(1,128)} %param.10) | copy-start | bytes 772
  88.1 11.9 %copy-start.4 = (f32[2,1]{0,1:T(1,128)S(1)}, f32[2,1]{0,1:T(1,128)}, u32[]{:S(2)}) copy-start(f32[2,1]{0,1:T(1,128)} %param.14) | copy-start | bytes 28
  95.3 11.0 %all-to-all-start.2 = ((f32[8,1,32]{2,1,0:T(1,128)}), f32[8,1,32]{2,1,0:T(1,128)S(1)}, u32[]{:S(2)}, u32[]{:S(2)}) async-start(f32[8,1,32]{2,1,0:T(1,128)} %all_to_all.27), calls=%async_computation.2 | async-start | bytes 8192 | tf_op jit(solution)/shard_map/all_to_all | solution.py:86
  177.0 52.1 %all-to-all-start.4 = ((bf16[8,32,4096]{2,1,0:T(8,128)(2,1)}), bf16[8,32,4096]{2,1,0:T(8,128)(2,1)}, u32[]{:S(2)}, u32[]{:S(2)}) async-start(bf16[8,32,4096]{2,1,0:T(8,128)(2,1)} %reshape.248), calls=%async_computation.4 | async-start | bytes 4194304 | tf_op jit(solution)/shard_map/all_to_all | solution.py:111
  214.0 19.8 %copy-start.1 = (bf16[2,1,32,128]{3,2,1,0:T(8,128)(2,1)S(1)}, bf16[2,1,32,128]{3,2,1,0:T(8,128)(2,1)}, u32[]{:S(2)}) copy-start(bf16[2,1,32,128]{3,2,1,0:T(8,128)(2,1)} %param.8) | copy-start | bytes 49156
where the time goes:
time: 237 us; the launch traced here: 235 us
  local copies, waits for them, and re-layouts  78.6 us (33%)
  matrix products  58 us (24%)
  blocking collectives  49.8 us (21%)
  starting transfers between devices  20.6 us (9%)
  other arithmetic  14 us (6%)
  waiting for transfers between devices  10.6 us (4%)
  between operations  3.39 us (1%)
    psum x1, blocking collectives, on_device(): lax.psum((jnp.sum(query_weights * divergence), jnp.sum(query_weights)), (...  38.7 us
    reshape x1, local copies, waits for them, and re-layouts, on_device(): blocks = blocks_flat.reshape(slot_count, token_len, feature_dim)  16.5 us
    convert_element_type x1, local copies, waits for them, and re-layouts, on_device(): returned = jnp.einsum('sij,sid->sjd', scaled_grad, got_queries, preferred...  16.4 us
    convert_element_type x1, local copies, waits for them, and re-layouts, on_device(): jnp.dot(pick_hot, flat_passages, preferred_element_type=jnp.float32)  16.2 us
    dot_general x1, matrix products, on_device(): jnp.einsum('sid,sjd->sij', got_queries, blocks, preferred_element_type=jn...  15.2 us
    dot_general x1, matrix products, on_device(): jnp.einsum('sij,sid->sjd', scaled_grad, got_queries, preferred_element_ty...  14.7 us
    all_to_all x1, blocking collectives, on_device(): lax.all_to_all(slot_score_grad.reshape(groups, capacity), 'grp', split_ax...  11.1 us
    unnamed x14, local copies, waits for them, and re-layouts  10.6 us
  transfers between devices with their start and end apart: 4, of which 3 were waited for; matrix products, arithmetic and copies ran while one was open for 41% of the time, Pallas kernels for 0%

commit v1 on v0

v1 whole, which is shorter than its diff:
```python
import functools
import math

import jax
import jax.numpy as jnp
from jax import lax
from jax.experimental import pallas as pl
from jax.experimental.pallas import tpu as pltpu
from jax.sharding import PartitionSpec as P

temper = 0.05
to_base2 = 1.0 / (temper * math.log(2.0))
LANES = 128
MESH = pl.DeviceIdType.MESH
HIGH = lax.Precision.HIGHEST
VMEM_SPEC = pl.BlockSpec(memory_space=pltpu.VMEM)


def greet(groups, replicas, me, mine):
    barrier = pltpu.get_barrier_semaphore()
    for step in range(1, groups):
        pl.semaphore_signal(
            barrier, inc=1, device_id={"grp": lax.rem(me + step, groups)}, device_id_type=MESH
        )
    for step in range(1, replicas):
        pl.semaphore_signal(
            barrier, inc=1, device_id={"rep": lax.rem(mine + step, replicas)}, device_id_type=MESH
        )
    pl.semaphore_wait(barrier, groups - 1 + replicas - 1)


def share_kernel(
    groups, block, queries_ref, cand_ref, map_ref, teacher_ref, weights_ref,
    all_queries, all_meta, query_buf, meta_buf, send_sem, recv_sem,
):
    me = lax.axis_index("grp")
    count, ways = cand_ref.shape
    table = map_ref[...].astype(jnp.float32)
    ids = lax.broadcasted_iota(jnp.int32, (ways, table.shape[1]), 1)
    diagonal = lax.broadcasted_iota(jnp.int32, (ways, ways), 0) == lax.broadcasted_iota(
        jnp.int32, (ways, ways), 1
    )
    teacher = teacher_ref[...]
    top = jnp.max(teacher, axis=1, keepdims=True)
    log_teacher = teacher - top
    log_teacher = log_teacher - jnp.log(jnp.sum(jnp.exp(log_teacher), axis=1, keepdims=True))
    prob = jnp.exp(log_teacher)
    entropy = jnp.sum(prob * log_teacher, axis=1, keepdims=True)
    meta_buf[me] = jnp.zeros(meta_buf.shape[1:], jnp.float32)
    for q in range(count):
        line = cand_ref[q : q + 1, :].astype(jnp.float32)
        column = jnp.sum(jnp.where(diagonal, line, 0.0), axis=1, keepdims=True).astype(jnp.int32)
        row = jnp.sum(jnp.where(column == ids, table, 0.0), axis=1, keepdims=True)
        row = jnp.sum(jnp.where(diagonal, row, 0.0), axis=0, keepdims=True)
        meta_buf[me, q : q + 1, :ways] = row
    meta_buf[me, count : 2 * count, :ways] = prob
    meta_buf[me, 2 * count : 3 * count, :] = jnp.broadcast_to(weights_ref[...], (count, LANES))
    meta_buf[me, 3 * count : 4 * count, :] = jnp.broadcast_to(entropy, (count, LANES))
    query_buf[me] = queries_ref[...]
    greet(groups, 1, me, 0)
    copies = []
    for step in range(1, groups):
        peer = lax.rem(me + step, groups)
        for which, buf in enumerate((query_buf, meta_buf)):
            copies.append(
                pltpu.make_async_remote_copy(
                    src_ref=buf.at[me],
                    dst_ref=buf.at[me],
                    send_sem=send_sem.at[which, step],
                    recv_sem=recv_sem.at[which, step],
                    device_id={"grp": peer},
                    device_id_type=MESH,
                )
            )
            copies[-1].start()
    for copy in copies:
        copy.wait()
    all_queries[...] = query_buf[...]
    all_meta[...] = meta_buf[...]


def forward_kernel(
    per_step, count, ways, block, lengths_ref, passages_ref, queries_ref, meta_ref,
    lse_ref, score_ref, hits_ref, mass_ref,
):
    step = pl.program_id(0)
    groups = meta_ref.shape[0]
    tokens = passages_ref.shape[1]
    slot = score_ref.shape[1]

    @pl.when(step == 0)
    def _():
        spots = lax.broadcasted_iota(jnp.int32, (ways, groups * slot), 1)
        for source in range(groups):
            turned = jnp.transpose(meta_ref[source])
            for q in range(count):
                row = turned[:ways, q : q + 1].astype(jnp.int32)
                spot = row + (slot - block) * (row // block)
                hot = spot == spots
                place = source * count + q
                hits_ref[place : place + 1, :] = jnp.sum(
                    jnp.where(hot, 1.0, 0.0), axis=0, keepdims=True
                )
                mass_ref[place : place + 1, :] = jnp.sum(
                    jnp.where(hot, turned[:ways, count + q : count + q + 1], 0.0),
                    axis=0,
                    keepdims=True,
                )

    position = lax.broadcasted_iota(jnp.int32, (tokens, 1), 0)
    for k in range(per_step):
        length = lengths_ref[step * per_step + k]
        products = lax.dot_general(
            passages_ref[k], queries_ref[...], (((1,), (1,)), ((), ())),
            preferred_element_type=jnp.float32,
        )
        scaled = jnp.where(position < length, products * to_base2, -1e30)
        highest = jnp.max(scaled, axis=0, keepdims=True)
        summed = jnp.sum(jnp.exp2(scaled - highest), axis=0, keepdims=True)
        lse_ref[step * per_step + k, :, :] = highest + jnp.log2(summed)

    @pl.when(step == pl.num_programs(0) - 1)
    def _():
        total, width = score_ref.shape[0], lse_ref.shape[2]
        each = width // total
        belongs = lax.broadcasted_iota(jnp.int32, (total, width), 1) // each
        pick = jnp.where(
            belongs == lax.broadcasted_iota(jnp.int32, (total, width), 0), 1.0, 0.0
        )
        matched = lse_ref[:, 0, :] * (1.0 / to_base2)
        score_ref[...] = jnp.zeros_like(score_ref)
        score_ref[:, : lse_ref.shape[0]] = lax.dot_general(
            pick, matched, (((1,), (1,)), ((), ())),
            precision=HIGH, preferred_element_type=jnp.float32,
        )


def grade_kernel(
    groups, replicas, score_ref, hits_ref, mass_ref, meta_ref, grad_ref, loss_ref,
    score_buf, weight_buf, grad_buf, query_weight, query_entropy,
    send_sem, recv_sem, wsend_sem, wrecv_sem,
):
    me = lax.axis_index("grp")
    mine = lax.axis_index("rep")
    total, slot = score_ref.shape
    count = total // groups
    for source in range(groups):
        span = slice(source * count, (source + 1) * count)
        query_weight[span, :] = meta_ref[source, 2 * count : 3 * count, :]
        query_entropy[span, :] = meta_ref[source, 3 * count : 4 * count, :]
    weights = query_weight[:, :1]
    score_buf[me] = score_ref[...]
    weight_buf[mine] = jnp.broadcast_to(
        jnp.sum(query_weight[...], axis=0, keepdims=True), weight_buf.shape[1:]
    )
    greet(groups, replicas, me, mine)
    copies = []
    for step in range(1, groups):
        copies.append(
            pltpu.make_async_remote_copy(
                src_ref=score_buf.at[me],
                dst_ref=score_buf.at[me],
                send_sem=send_sem.at[step],
                recv_sem=recv_sem.at[step],
                device_id={"grp": lax.rem(me + step, groups)},
                device_id_type=MESH,
            )
        )
        copies[-1].start()
    for step in range(1, replicas):
        copies.append(
            pltpu.make_async_remote_copy(
                src_ref=weight_buf.at[mine],
                dst_ref=weight_buf.at[mine],
                send_sem=wsend_sem.at[step],
                recv_sem=wrecv_sem.at[step],
                device_id={"rep": lax.rem(mine + step, replicas)},
                device_id_type=MESH,
            )
        )
        copies[-1].start()
    for copy in copies:
        copy.wait()
    weight_sum = jnp.sum(weight_buf[...], axis=0)[:1, :1]
    scores = jnp.concatenate([score_buf[owner] for owner in range(groups)], axis=1)
    hits = hits_ref[...]
    mass = mass_ref[...]
    asked = hits > 0.0
    held = jnp.where(asked, scores, -1e30)
    highest = jnp.max(held, axis=1, keepdims=True)
    summed = jnp.sum(hits * jnp.exp(held - highest), axis=1, keepdims=True)
    log_student = jnp.where(asked, scores - (highest + jnp.log(summed)), -1e30)
    student = hits * jnp.exp(log_student)
    crossed = jnp.sum(jnp.where(asked, mass * log_student, 0.0), axis=1, keepdims=True)
    divergence = query_entropy[:, :1] - crossed
    grad_buf[...] = (total * replicas) * weights / weight_sum * (student - mass)
    own = grad_buf[:, pl.ds(pl.multiple_of(me * slot, slot), slot)]
    width = grad_ref.shape[2]
    each = width // total
    belongs = lax.broadcasted_iota(jnp.int32, (total, width), 1) // each
    pick = jnp.where(belongs == lax.broadcasted_iota(jnp.int32, (total, width), 0), 1.0, 0.0)
    spread = lax.dot_general(
        own, pick, (((0,), (0,)), ((), ())), precision=HIGH, preferred_element_type=jnp.float32
    )
    grad_ref[:, 0, :] = spread[: grad_ref.shape[0]]
    loss_ref[...] = jnp.broadcast_to(
        jnp.sum(weights * divergence, axis=0, keepdims=True) / weight_sum, loss_ref.shape
    )


def backward_kernel(
    per_step, lengths_ref, passages_ref, queries_ref, lse_ref, grad_ref, out_ref, partial_ref, total
):
    step = pl.program_id(0)
    tokens = passages_ref.shape[1]

    @pl.when(step == 0)
    def _():
        total[...] = jnp.zeros_like(total)

    position = lax.broadcasted_iota(jnp.int32, (tokens, 1), 0)
    queries = queries_ref[...]
    added = None
    for k in range(per_step):
        usable = position < lengths_ref[step * per_step + k]
        passage = passages_ref[k]
        products = lax.dot_general(
            passage, queries, (((1,), (1,)), ((), ())), preferred_element_type=jnp.float32
        )
        powers = jnp.exp2(jnp.minimum(products * to_base2 - lse_ref[k], 0.0))
        scaled_grad = (powers * grad_ref[k]).astype(jnp.bfloat16)
        token_grad = jnp.dot(scaled_grad, queries, preferred_element_type=jnp.float32)
        out_ref[k] = jnp.where(usable, token_grad, 0.0).astype(jnp.bfloat16)
        kept = jnp.where(usable, passage.astype(jnp.float32), 0.0).astype(jnp.bfloat16)
        part = lax.dot_general(
            scaled_grad, kept, (((0,), (0,)), ((), ())), preferred_element_type=jnp.float32
        )
        added = part if added is None else added + part
    total[...] += added

    @pl.when(step == pl.num_programs(0) - 1)
    def _():
        partial_ref[...] = total[...].astype(partial_ref.dtype)


def collect_kernel(
    groups, replicas, partial_ref, loss_ref, grad_ref, loss_out,
    arrived, loss_buf, send_sem, recv_sem, lsend_sem, lrecv_sem,
):
    me = lax.axis_index("grp")
    mine = lax.axis_index("rep")
    loss_buf[mine] = loss_ref[...]
    greet(groups, replicas, me, mine)
    copies = []
    for step in range(1, groups):
        peer = lax.rem(me + step, groups)
        copies.append(
            pltpu.make_async_remote_copy(
                src_ref=partial_ref.at[peer],
                dst_ref=arrived.at[me],
                send_sem=send_sem.at[step],
                recv_sem=recv_sem.at[step],
                device_id={"grp": peer},
                device_id_type=MESH,
            )
        )
        copies[-1].start()
    for step in range(1, replicas):
        copies.append(
            pltpu.make_async_remote_copy(
                src_ref=loss_buf.at[mine],
                dst_ref=loss_buf.at[mine],
                send_sem=lsend_sem.at[step],
                recv_sem=lrecv_sem.at[step],
                device_id={"rep": lax.rem(mine + step, replicas)},
                device_id_type=MESH,
            )
        )
        copies[-1].start()
    arrived[me] = partial_ref[me]
    for copy in copies:
        copy.wait()
    grad_ref[...] = jnp.sum(arrived[...].astype(jnp.float32), axis=0)
    loss_out[...] = jnp.sum(loss_buf[...], axis=0)


def on_device(queries, passages, lengths, cand_ids, owner_map, teacher, weights):
    groups = lax.axis_size("grp")
    replicas = lax.axis_size("rep")
    count, _, query_len, dim = queries.shape
    block, _, tokens, _ = passages.shape
    ways = cand_ids.shape[2]
    own_rows = count * query_len
    width = groups * own_rows
    total = groups * count
    slot = -(-block // LANES) * LANES
    f32 = jnp.float32
    dma = pltpu.SemaphoreType.DMA
    meta_rows = -(-4 * count // 8) * 8
    all_queries, all_meta = pl.pallas_call(
        functools.partial(share_kernel, groups, block),
        name="share",
        out_shape=[
            jax.ShapeDtypeStruct((groups, own_rows, dim), queries.dtype),
            jax.ShapeDtypeStruct((groups, meta_rows, LANES), f32),
        ],
        in_specs=[VMEM_SPEC] * 5,
        out_specs=[VMEM_SPEC] * 2,
        scratch_shapes=[
            pltpu.VMEM((groups, own_rows, dim), queries.dtype),
            pltpu.VMEM((groups, meta_rows, LANES), f32),
            dma((2, groups)),
            dma((2, groups)),
        ],
        compiler_params=pltpu.CompilerParams(collective_id=0, has_side_effects=True),
    )(
        queries.reshape(own_rows, dim),
        cand_ids[:, 0],
        owner_map,
        teacher[:, 0],
        weights,
    )
    flat_queries = all_queries.reshape(width, dim)
    flat_passages = passages.reshape(block, tokens, dim)
    flat_lengths = lengths.reshape(block)
    per_step = 4 if block % 4 == 0 else 1
    steps = block // per_step
    whole = lambda *shape: pl.BlockSpec(shape, lambda i, *_: (0,) * len(shape))
    passage_spec = pl.BlockSpec((per_step, tokens, dim), lambda i, *_: (i, 0, 0))
    row_spec = pl.BlockSpec((per_step, 1, width), lambda i, *_: (i, 0, 0))
    lse, score, hits, mass = pl.pallas_call(
        functools.partial(forward_kernel, per_step, count, ways, block),
        name="forward",
        grid_spec=pltpu.PrefetchScalarGridSpec(
            num_scalar_prefetch=1,
            grid=(steps,),
            in_specs=[passage_spec, whole(width, dim), whole(groups, meta_rows, LANES)],
            out_specs=[
                whole(block, 1, width),
                whole(total, slot),
                whole(total, groups * slot),
                whole(total, groups * slot),
            ],
        ),
        out_shape=[
            jax.ShapeDtypeStruct((block, 1, width), f32),
            jax.ShapeDtypeStruct((total, slot), f32),
            jax.ShapeDtypeStruct((total, groups * slot), f32),
            jax.ShapeDtypeStruct((total, groups * slot), f32),
        ],
        compiler_params=pltpu.CompilerParams(dimension_semantics=("arbitrary",)),
    )(flat_lengths, flat_passages, flat_queries, all_meta)
    grad, loss_part = pl.pallas_call(
        functools.partial(grade_kernel, groups, replicas),
        name="grade",
        out_shape=[
            jax.ShapeDtypeStruct((block, 1, width), f32),
            jax.ShapeDtypeStruct((8, LANES), f32),
        ],
        in_specs=[VMEM_SPEC] * 4,
        out_specs=[VMEM_SPEC] * 2,
        scratch_shapes=[
            pltpu.VMEM((groups, total, slot), f32),
            pltpu.VMEM((replicas, 8, LANES), f32),
            pltpu.VMEM((total, groups * slot), f32),
            pltpu.VMEM((total, LANES), f32),
            pltpu.VMEM((total, LANES), f32),
            dma((groups,)),
            dma((groups,)),
            dma((replicas,)),
            dma((replicas,)),
        ],
        compiler_params=pltpu.CompilerParams(collective_id=1, has_side_effects=True),
    )(score, hits, mass, all_meta)
    passage_grad, partial = pl.pallas_call(
        functools.partial(backward_kernel, per_step),
        name="backward",
        grid_spec=pltpu.PrefetchScalarGridSpec(
            num_scalar_prefetch=1,
            grid=(steps,),
            in_specs=[passage_spec, whole(width, dim), row_spec, row_spec],
            out_specs=[passage_spec, whole(width, dim)],
            scratch_shapes=[pltpu.VMEM((width, dim), f32)],
        ),
        out_shape=[
            jax.ShapeDtypeStruct((block, tokens, dim), jnp.bfloat16),
            jax.ShapeDtypeStruct((width, dim), jnp.bfloat16),
        ],
        compiler_params=pltpu.CompilerParams(dimension_semantics=("arbitrary",)),
    )(flat_lengths, flat_passages, flat_queries, lse, grad)
    query_grad, loss = pl.pallas_call(
        functools.partial(collect_kernel, groups, replicas),
        name="collect",
        out_shape=[
            jax.ShapeDtypeStruct((own_rows, dim), f32),
            jax.ShapeDtypeStruct((8, LANES), f32),
        ],
        in_specs=[VMEM_SPEC] * 2,
        out_specs=[VMEM_SPEC] * 2,
        scratch_shapes=[
            pltpu.VMEM((groups, own_rows, dim), jnp.bfloat16),
            pltpu.VMEM((replicas, 8, LANES), f32),
            dma((groups,)),
            dma((groups,)),
            dma((replicas,)),
            dma((replicas,)),
        ],
        compiler_params=pltpu.CompilerParams(collective_id=2, has_side_effects=True),
    )(partial.reshape(groups, own_rows, dim), loss_part)
    return (
        loss[0, 0],
        query_grad.reshape(count, 1, query_len, dim),
        passage_grad.reshape(block, 1, tokens, dim),
    )


def solution(mesh):
    return jax.shard_map(
        on_device,
        mesh=mesh,
        in_specs=(
            P("grp", "rep", None, None),
            P("grp", "rep", None, None),
            P("grp", "rep"),
            P("grp", "rep", None),
            P("rep", None),
            P("grp", "rep", None),
            P("grp", "rep"),
        ),
        out_specs=(P(), P("grp", "rep", None, None), P("grp", "rep", None, None)),
        check_vma=False,
    )
```

time: 237 us -> 84.4 us (0.36)
  Pallas kernels: 0 us -> 70.3 us
  local copies, waits for them, and re-layouts: 78.6 us -> 12.7 us
  matrix products: 58 us -> 0 us
  blocking collectives: 49.8 us -> 0 us
  starting transfers between devices: 20.6 us -> 0 us
  other arithmetic: 14 us -> 0 us
  waiting for transfers between devices: 10.6 us -> 0 us
  between operations: 3.39 us -> 0.67 us
    pallas_call x0 -> x5, Pallas kernels: none -> 70.3 us  [the longest x1 23.6 us: on_device(): pl.pallas_call(functools.partial(backward_kernel, per_step), name='backwa...]
    dot_general x7 -> x0, matrix products: 58 us -> none  [the longest x1 15.2 us: on_device(): jnp.einsum('sid,sjd->sij', got_queries, blocks, preferred_element_type=jn...]
    psum x1 -> x0, blocking collectives: 38.7 us -> none  [on_device(): lax.psum((jnp.sum(query_weights * divergence), jnp.sum(query_weights)), (...]
    convert_element_type x2 -> x0, local copies, waits for them, and re-layouts: 32.7 us -> none  [the longest x1 16.4 us: on_device(): returned = jnp.einsum('sij,sid->sjd', scaled_grad, got_queries, preferred...]
    reshape x8 -> x0, local copies, waits for them, and re-layouts: 27.2 us -> none  [the longest x1 16.5 us: on_device(): blocks = blocks_flat.reshape(slot_count, token_len, feature_dim)]
    all_to_all x4 -> x0, starting transfers between devices: 20.6 us -> none  [the longest x1 7.31 us: on_device(): lax.all_to_all(request.reshape(groups, capacity), 'grp', split_axis=0, co...]
    all_to_all x1 -> x0, blocking collectives: 11.1 us -> none  [on_device(): lax.all_to_all(slot_score_grad.reshape(groups, capacity), 'grp', split_ax...]
    all_to_all x4 -> x0, waiting for transfers between devices: 10.6 us -> none  [the longest x1 5.78 us: on_device(): lax.all_to_all(slot_scores.reshape(groups, capacity), 'grp', split_axis=0...]
  transfers between devices with their start and end apart: 4 -> 0, of which waited for: 3 -> 0; matrix products, arithmetic and copies ran while one was open for 41% -> 0% of each run, Pallas kernels for 0% -> 0%
where the time goes in v1:
time: 84.4 us; the launch traced here: 83.7 us
  Pallas kernels  70.3 us (83%)
  local copies, waits for them, and re-layouts  12.7 us (15%)
    pallas_call x1, Pallas kernels, on_device(): pl.pallas_call(functools.partial(backward_kernel, per_step), name='backwa...  23.6 us
    pallas_call x1, Pallas kernels, on_device(): pl.pallas_call(functools.partial(forward_kernel, per_step, count, ways, b...  16.3 us
    unnamed x6, local copies, waits for them, and re-layouts  11.5 us
    pallas_call x1, Pallas kernels, on_device(): pl.pallas_call(functools.partial(share_kernel, groups, block), name='shar...  11.4 us
    pallas_call x1, Pallas kernels, on_device(): pl.pallas_call(functools.partial(grade_kernel, groups, replicas), name='g...  10.2 us
    pallas_call x1, Pallas kernels, on_device(): pl.pallas_call(functools.partial(collect_kernel, groups, replicas), name=...  8.82 us

profile of v1, /device:TPU:0, one launch (start us, length us, event | category | flops | bytes accessed | tf_op | source)
XLA Modules:
  0.0 83.7 jit_solution(5331212124533928331)
XLA Ops:
  0.6 1.3 %copy.11.weights_ref = f32[2,1]{1,0:T(2,128)} copy(f32[2,1]{0,1:T(1,128)} %param.13) | data formatting | bytes 16 | tf_op args[6]
  1.9 11.4 %share.1 = (bf16[8,64,128]{2,1,0:T(8,128)(2,1)}, f32[8,8,128]{2,1,0:T(8,128)}) custom-call(bf16[64,128]{1,0:T(8,128)(2,1)} %bitcast.21, s32[2,64]{1,0:T(2,128)} %bitcast.24, s32[1,512]{1,0:T(1,128)} %map_ref.1, f32[2,64]{1,0:T(2,128)} %bitcast.25, f32[2,1]{1,0:T(2,128)} %copy.11.weights_ref), custom_call_target="tpu_custom_call" | custom-call | tf_op jit(solution)/shard_map/share/pallas_call | solution.py:300
  13.4 5.4 %copy.15 = bf16[64,1,180,128]{3,2,0,1:T(8,128)(2,1)} copy(bf16[64,1,180,128]{3,0,2,1:T(8,128)(2,1)} %param.8) | data formatting | bytes 5898240 | tf_op args[1]
  18.7 16.3 %forward.1 = (f32[64,1,512]{2,1,0:T(1,128)}, f32[16,128]{1,0:T(8,128)}, f32[16,1024]{1,0:T(8,128)}, f32[16,1024]{1,0:T(8,128)}) custom-call(s32[64]{0:T(128)} %bitcast.22, bf16[64,180,128]{2,1,0:T(8,128)(2,1)} %bitcast.14, bf16[512,128]{1,0:T(8,128)(2,1)} %bitcast.17, f32[8,8,128]{2,1,0:T(8,128)} %get-tuple-element.16.meta_ref), custom_call_target="tpu_custom_call" | custom-call | tf_op jit(solution)/shard_map/forward/pallas_call | solution.py:331
  35.0 10.2 %grade.1 = (f32[64,1,512]{2,1,0:T(1,128)}, f32[8,128]{1,0:T(8,128)}) custom-call(f32[16,128]{1,0:T(8,128)} %get-tuple-element.18.score_ref, f32[16,1024]{1,0:T(8,128)} %get-tuple-element.19.hits_ref, f32[16,1024]{1,0:T(8,128)} %get-tuple-element.20.mass_ref, f32[8,8,128]{2,1,0:T(8,128)} %get-tuple-element.16.meta_ref), custom_call_target="tpu_custom_call" | custom-call | tf_op jit(solution)/shard_map/grade/pallas_call | solution.py:353
  45.2 23.6 %backward.1 = (bf16[64,180,128]{2,1,0:T(8,128)(2,1)}, bf16[512,128]{1,0:T(8,128)(2,1)}) custom-call(s32[64]{0:T(128)} %bitcast.23, bf16[64,180,128]{2,1,0:T(8,128)(2,1)} %bitcast.15, bf16[512,128]{1,0:T(8,128)(2,1)} %bitcast.18, f32[64,1,512]{2,1,0:T(1,128)} %get-tuple-element.17.lse_ref, f32[64,1,512]{2,1,0:T(1,128)} %get-tuple-element.21.grad_ref), custom_call_target="tpu_custom_call" | custom-call | tf_op jit(solution)/shard_map/backward/pallas_call | solution.py:375
  68.8 8.8 %collect.1 = (f32[64,128]{1,0:T(8,128)}, f32[8,128]{1,0:T(8,128)}) custom-call(bf16[8,64,128]{2,1,0:T(8,128)(2,1)} %bitcast.19, f32[8,128]{1,0:T(8,128)} %get-tuple-element.23.loss_ref), custom_call_target="tpu_custom_call" | custom-call | tf_op jit(solution)/shard_map/collect/pallas_call | solution.py:391
  77.7 0.0 copy-start
  77.7 1.2 %slice.3 = f32[1,1]{1,0:T(1,128)} slice(f32[8,128]{1,0:T(8,128)} %get-tuple-element.24), slice={[0:1], [0:1]} | slice | bytes 8 | tf_op jit(solution)/shard_map/slice | solution.py:411
  78.9 4.2 %copy.13 = bf16[64,1,180,128]{3,0,2,1:T(8,128)(2,1)} copy(bf16[64,1,180,128]{3,2,0,1:T(8,128)(2,1)} %bitcast.16) | data formatting | bytes 5898240
  83.1 0.0 copy-done
  83.1 0.6 copy.17
Async XLA Ops:
  77.7 5.5 %copy-start = (f32[64,128]{1,0:T(8,128)S(1)}, f32[64,128]{1,0:T(8,128)}, u32[]{:S(2)}) copy-start(f32[64,128]{1,0:T(8,128)} %get-tuple-element.25) | copy-start | bytes 98308

commit v2 on v1

--- a/solution.py
+++ b/solution.py
@@ -79,16 +79,30 @@
     all_meta[...] = meta_buf[...]
 
 
+def span_of(tokens, limit):
+    return max(size for size in range(1, limit + 1) if tokens % size == 0)
+
+
+def lengths_of(lengths_ref, first, rows, width):
+    index = lax.broadcasted_iota(jnp.int32, (rows, width), 0)
+    found = jnp.zeros((rows, width), jnp.int32)
+    for k in range(rows):
+        found = jnp.where(index == k, lengths_ref[first + k], found)
+    return found
+
+
 def forward_kernel(
-    per_step, count, ways, block, lengths_ref, passages_ref, queries_ref, meta_ref,
-    lse_ref, score_ref, hits_ref, mass_ref,
+    count, ways, block, lengths_ref, passages_ref, queries_ref, meta_ref,
+    lse_ref, score_ref, hits_ref, mass_ref, held, all_lse,
 ):
     step = pl.program_id(0)
+    part = pl.program_id(1)
     groups = meta_ref.shape[0]
-    tokens = passages_ref.shape[1]
+    tokens, rows, dim = passages_ref.shape
+    width = queries_ref.shape[0]
     slot = score_ref.shape[1]
 
-    @pl.when(step == 0)
+    @pl.when((step == 0) & (part == 0))
     def _():
         spots = lax.broadcasted_iota(jnp.int32, (ways, groups * slot), 1)
         for source in range(groups):
@@ -107,32 +121,46 @@
                     keepdims=True,
                 )
 
-    position = lax.broadcasted_iota(jnp.int32, (tokens, 1), 0)
-    for k in range(per_step):
-        length = lengths_ref[step * per_step + k]
+    lengths = lengths_of(lengths_ref, step * rows, rows, width)
+    size = span_of(tokens, 20)
+    highest = jnp.full((rows, width), -1e30, jnp.float32)
+    for first in range(0, tokens, size):
         products = lax.dot_general(
-            passages_ref[k], queries_ref[...], (((1,), (1,)), ((), ())),
-            preferred_element_type=jnp.float32,
-        )
-        scaled = jnp.where(position < length, products * to_base2, -1e30)
-        highest = jnp.max(scaled, axis=0, keepdims=True)
-        summed = jnp.sum(jnp.exp2(scaled - highest), axis=0, keepdims=True)
-        lse_ref[step * per_step + k, :, :] = highest + jnp.log2(summed)
-
-    @pl.when(step == pl.num_programs(0) - 1)
+            passages_ref[first : first + size].reshape(size * rows, dim), queries_ref[...],
+            (((1,), (1,)), ((), ())), preferred_element_type=jnp.float32,
+        )
+        for j in range(size):
+            scaled = jnp.where(
+                first + j < lengths, products[j * rows : (j + 1) * rows] * to_base2, -1e30
+            )
+            held[first + j] = scaled
+            highest = jnp.maximum(highest, scaled)
+    summed = jnp.zeros((rows, width), jnp.float32)
+    for j in range(tokens):
+        summed = summed + jnp.exp2(held[j] - highest)
+    lse = highest + jnp.log2(summed)
+    lse_ref[...] = lse
+    all_lse[step, part] = lse
+
+    @pl.when((step == pl.num_programs(0) - 1) & (part == pl.num_programs(1) - 1))
     def _():
-        total, width = score_ref.shape[0], lse_ref.shape[2]
-        each = width // total
-        belongs = lax.broadcasted_iota(jnp.int32, (total, width), 1) // each
+        total = score_ref.shape[0]
+        parts = all_lse.shape[1]
+        each = width * parts // total
+        score_ref[...] = jnp.zeros_like(score_ref)
+        belongs = lax.broadcasted_iota(jnp.int32, (total // parts, width), 1) // each
         pick = jnp.where(
-            belongs == lax.broadcasted_iota(jnp.int32, (total, width), 0), 1.0, 0.0
-        )
-        matched = lse_ref[:, 0, :] * (1.0 / to_base2)
-        score_ref[...] = jnp.zeros_like(score_ref)
-        score_ref[:, : lse_ref.shape[0]] = lax.dot_general(
-            pick, matched, (((1,), (1,)), ((), ())),
-            precision=HIGH, preferred_element_type=jnp.float32,
-        )
+            belongs == lax.broadcasted_iota(jnp.int32, (total // parts, width), 0), 1.0, 0.0
+        )
+        span = total // parts
+        for k in range(parts):
+            matched = jnp.concatenate(
+                [all_lse[i, k] for i in range(all_lse.shape[0])], axis=0
+            ) * (1.0 / to_base2)
+            score_ref[k * span : (k + 1) * span, :block] = lax.dot_general(
+                pick, matched, (((1,), (1,)), ((), ())),
+                precision=HIGH, preferred_element_type=jnp.float32,
+            )
 
 
 def grade_kernel(
@@ -195,52 +223,77 @@
     divergence = query_entropy[:, :1] - crossed
     grad_buf[...] = (total * replicas) * weights / weight_sum * (student - mass)
     own = grad_buf[:, pl.ds(pl.multiple_of(me * slot, slot), slot)]
-    width = grad_ref.shape[2]
+    width = grad_ref.shape[1]
     each = width // total
     belongs = lax.broadcasted_iota(jnp.int32, (total, width), 1) // each
     pick = jnp.where(belongs == lax.broadcasted_iota(jnp.int32, (total, width), 0), 1.0, 0.0)
     spread = lax.dot_general(
         own, pick, (((0,), (0,)), ((), ())), precision=HIGH, preferred_element_type=jnp.float32
     )
-    grad_ref[:, 0, :] = spread[: grad_ref.shape[0]]
+    grad_ref[...] = spread[: grad_ref.shape[0]]
     loss_ref[...] = jnp.broadcast_to(
         jnp.sum(weights * divergence, axis=0, keepdims=True) / weight_sum, loss_ref.shape
     )
 
 
 def backward_kernel(
-    per_step, lengths_ref, passages_ref, queries_ref, lse_ref, grad_ref, out_ref, partial_ref, total
+    lengths_ref, passages_ref, queries_ref, lse_ref, grad_ref, out_ref, partial_ref,
+    total, token_total,
 ):
     step = pl.program_id(0)
-    tokens = passages_ref.shape[1]
+    part = pl.program_id(1)
+    parts = total.shape[0]
+    tokens, rows, dim = passages_ref.shape
+    width = queries_ref.shape[0]
 
     @pl.when(step == 0)
     def _():
-        total[...] = jnp.zeros_like(total)
-
-    position = lax.broadcasted_iota(jnp.int32, (tokens, 1), 0)
+        total[part] = jnp.zeros(total.shape[1:], jnp.float32)
+
+    if parts > 1:
+
+        @pl.when(part == 0)
+        def _():
+            token_total[...] = jnp.zeros_like(token_total)
+
+    lengths = lengths_of(lengths_ref, step * rows, rows, width)[None]
+    lse = lse_ref[...][None]
+    grad = grad_ref[...][None]
     queries = queries_ref[...]
+    size = span_of(tokens, 36)
     added = None
-    for k in range(per_step):
-        usable = position < lengths_ref[step * per_step + k]
-        passage = passages_ref[k]
+    for first in range(0, tokens, size):
+        passage = passages_ref[first : first + size].reshape(size * rows, dim)
         products = lax.dot_general(
             passage, queries, (((1,), (1,)), ((), ())), preferred_element_type=jnp.float32
-        )
-        powers = jnp.exp2(jnp.minimum(products * to_base2 - lse_ref[k], 0.0))
-        scaled_grad = (powers * grad_ref[k]).astype(jnp.bfloat16)
-        token_grad = jnp.dot(scaled_grad, queries, preferred_element_type=jnp.float32)
-        out_ref[k] = jnp.where(usable, token_grad, 0.0).astype(jnp.bfloat16)
-        kept = jnp.where(usable, passage.astype(jnp.float32), 0.0).astype(jnp.bfloat16)
-        part = lax.dot_general(
-            scaled_grad, kept, (((0,), (0,)), ((), ())), preferred_element_type=jnp.float32
-        )
-        added = part if added is None else added + part
-    total[...] += added
+        ).reshape(size, rows, width)
+        position = first + lax.broadcasted_iota(jnp.int32, (size, 1, 1), 0)
+        powers = jnp.exp2(jnp.where(position < lengths, products * to_base2 - lse, -1e30))
+        scaled_grad = (powers * grad).astype(jnp.bfloat16).reshape(size * rows, width)
+        token_grad = jnp.dot(scaled_grad, queries, preferred_element_type=jnp.float32).reshape(
+            size, rows, dim
+        )
+        if parts > 1:
+            token_total[first : first + size] += token_grad
+        else:
+            out_ref[first : first + size] = token_grad.astype(jnp.bfloat16)
+        piece = lax.dot_general(
+            passage, scaled_grad, (((0,), (0,)), ((), ())), preferred_element_type=jnp.float32
+        )
+        added = piece if added is None else added + piece
+    total[part] += added
+
+    if parts > 1:
+
+        @pl.when(part == parts - 1)
+        def _():
+            out_ref[...] = token_total[...].astype(jnp.bfloat16)
 
     @pl.when(step == pl.num_programs(0) - 1)
     def _():
-        partial_ref[...] = total[...].astype(partial_ref.dtype)
+        partial_ref[pl.ds(pl.multiple_of(part * width, width), width), :] = jnp.transpose(
+            total[part]
+        ).astype(partial_ref.dtype)
 
 
 def collect_kernel(
@@ -321,40 +374,48 @@
         weights,
     )
     flat_queries = all_queries.reshape(width, dim)
-    flat_passages = passages.reshape(block, tokens, dim)
+    flat_passages = jnp.transpose(passages[:, 0], (1, 0, 2))
     flat_lengths = lengths.reshape(block)
-    per_step = 4 if block % 4 == 0 else 1
-    steps = block // per_step
-    whole = lambda *shape: pl.BlockSpec(shape, lambda i, *_: (0,) * len(shape))
-    passage_spec = pl.BlockSpec((per_step, tokens, dim), lambda i, *_: (i, 0, 0))
-    row_spec = pl.BlockSpec((per_step, 1, width), lambda i, *_: (i, 0, 0))
+    rows = 16 if block % 16 == 0 else block
+    chunk = width if width <= 512 else width // (width // 512)
+    parts = width // chunk
+    grid = (block // rows, parts)
+    whole = lambda *shape: pl.BlockSpec(shape, lambda i, k, *_: (0,) * len(shape))
+    passage_spec = pl.BlockSpec((tokens, rows, dim), lambda i, k, *_: (0, i, 0))
+    query_spec = pl.BlockSpec((chunk, dim), lambda i, k, *_: (k, 0))
+    row_spec = pl.BlockSpec((rows, chunk), lambda i, k, *_: (i, k))
+    both = pltpu.CompilerParams(dimension_semantics=("arbitrary", "arbitrary"))
     lse, score, hits, mass = pl.pallas_call(
-        functools.partial(forward_kernel, per_step, count, ways, block),
+        functools.partial(forward_kernel, count, ways, block),
         name="forward",
         grid_spec=pltpu.PrefetchScalarGridSpec(
             num_scalar_prefetch=1,
-            grid=(steps,),
-            in_specs=[passage_spec, whole(width, dim), whole(groups, meta_rows, LANES)],
+            grid=grid,
+            in_specs=[passage_spec, query_spec, whole(groups, meta_rows, LANES)],
             out_specs=[
-                whole(block, 1, width),
+                row_spec,
                 whole(total, slot),
                 whole(total, groups * slot),
                 whole(total, groups * slot),
             ],
+            scratch_shapes=[
+                pltpu.VMEM((tokens, rows, chunk), f32),
+                pltpu.VMEM((*grid, rows, chunk), f32),
+            ],
         ),
         out_shape=[
-            jax.ShapeDtypeStruct((block, 1, width), f32),
+            jax.ShapeDtypeStruct((block, width), f32),
             jax.ShapeDtypeStruct((total, slot), f32),
             jax.ShapeDtypeStruct((total, groups * slot), f32),
             jax.ShapeDtypeStruct((total, groups * slot), f32),
         ],
-        compiler_params=pltpu.CompilerParams(dimension_semantics=("arbitrary",)),
+        compiler_params=both,
     )(flat_lengths, flat_passages, flat_queries, all_meta)
     grad, loss_part = pl.pallas_call(
         functools.partial(grade_kernel, groups, replicas),
         name="grade",
         out_shape=[
-            jax.ShapeDtypeStruct((block, 1, width), f32),
+            jax.ShapeDtypeStruct((block, width), f32),
             jax.ShapeDtypeStruct((8, LANES), f32),
         ],
         in_specs=[VMEM_SPEC] * 4,
@@ -373,20 +434,23 @@
         compiler_params=pltpu.CompilerParams(collective_id=1, has_side_effects=True),
     )(score, hits, mass, all_meta)
     passage_grad, partial = pl.pallas_call(
-        functools.partial(backward_kernel, per_step),
+        backward_kernel,
         name="backward",
         grid_spec=pltpu.PrefetchScalarGridSpec(
             num_scalar_prefetch=1,
-            grid=(steps,),
-            in_specs=[passage_spec, whole(width, dim), row_spec, row_spec],
+            grid=grid,
+            in_specs=[passage_spec, query_spec, row_spec, row_spec],
             out_specs=[passage_spec, whole(width, dim)],
-            scratch_shapes=[pltpu.VMEM((width, dim), f32)],
+            scratch_shapes=[
+                pltpu.VMEM((parts, dim, chunk), f32),
+                pltpu.VMEM((tokens, rows, dim) if parts > 1 else (8, rows, dim), f32),
+            ],
         ),
         out_shape=[
-            jax.ShapeDtypeStruct((block, tokens, dim), jnp.bfloat16),
+            jax.ShapeDtypeStruct((tokens, block, dim), jnp.bfloat16),
             jax.ShapeDtypeStruct((width, dim), jnp.bfloat16),
         ],
-        compiler_params=pltpu.CompilerParams(dimension_semantics=("arbitrary",)),
+        compiler_params=both,
     )(flat_lengths, flat_passages, flat_queries, lse, grad)
     query_grad, loss = pl.pallas_call(
         functools.partial(collect_kernel, groups, replicas),
@@ -410,7 +474,7 @@
     return (
         loss[0, 0],
         query_grad.reshape(count, 1, query_len, dim),
-        passage_grad.reshape(block, 1, tokens, dim),
+        jnp.transpose(passage_grad, (1, 0, 2))[:, None],
     )
 
 

time: 84.4 us -> 61.5 us (0.73)
  Pallas kernels: 70.3 us -> 56.5 us
  local copies, waits for them, and re-layouts: 12.7 us -> 3.86 us
    pallas_call x2, Pallas kernels: 39.9 us -> 26.1 us  [the longest x1 14.1 us: on_device(): pl.pallas_call(backward_kernel, name='backward', grid_spec=pltpu.Prefetch...]
    unnamed x6 -> x2, local copies, waits for them, and re-layouts: 11.5 us -> 2.67 us
where the time goes in v2:
time: 61.5 us; the launch traced here: 61.1 us
  Pallas kernels  56.5 us (92%)
  local copies, waits for them, and re-layouts  3.86 us (6%)
  between operations  0.66 us (1%)
    pallas_call x1, Pallas kernels, on_device(): pl.pallas_call(backward_kernel, name='backward', grid_spec=pltpu.Prefetch...  14.1 us
    pallas_call x1, Pallas kernels, on_device(): pl.pallas_call(functools.partial(forward_kernel, count, ways, block), nam...  12 us
    pallas_call x1, Pallas kernels, on_device(): pl.pallas_call(functools.partial(share_kernel, groups, block), name='shar...  11.4 us
    pallas_call x1, Pallas kernels, on_device(): pl.pallas_call(functools.partial(grade_kernel, groups, replicas), name='g...  10.2 us
    pallas_call x1, Pallas kernels, on_device(): pl.pallas_call(functools.partial(collect_kernel, groups, replicas), name=...  8.82 us
    unnamed x2, local copies, waits for them, and re-layouts  2.67 us

profile of v2, /device:TPU:0, one launch (start us, length us, event | category | flops | bytes accessed | tf_op | source)
XLA Modules:
  0.0 61.1 jit_solution(13444086865572368655)
XLA Ops:
  0.6 1.3 %copy.10.weights_ref = f32[2,1]{1,0:T(2,128)} copy(f32[2,1]{0,1:T(1,128)} %param.13) | data formatting | bytes 16 | tf_op args[6]
  1.9 11.4 %share.1 = (bf16[8,64,128]{2,1,0:T(8,128)(2,1)}, f32[8,8,128]{2,1,0:T(8,128)}) custom-call(bf16[64,128]{1,0:T(8,128)(2,1)} %bitcast.22, s32[2,64]{1,0:T(2,128)} %bitcast.25, s32[1,512]{1,0:T(1,128)} %map_ref.1, f32[2,64]{1,0:T(2,128)} %bitcast.26, f32[2,1]{1,0:T(2,128)} %copy.10.weights_ref), custom_call_target="tpu_custom_call" | custom-call | tf_op jit(solution)/shard_map/share/pallas_call | solution.py:353
  13.4 12.0 %forward.1 = (f32[64,512]{1,0:T(8,128)}, f32[16,128]{1,0:T(8,128)}, f32[16,1024]{1,0:T(8,128)}, f32[16,1024]{1,0:T(8,128)}) custom-call(s32[64]{0:T(128)} %bitcast.23, bf16[180,64,128]{2,1,0:T(8,128)(2,1)} %bitcast.16, bf16[512,128]{1,0:T(8,128)(2,1)} %bitcast.18, f32[8,8,128]{2,1,0:T(8,128)} %get-tuple-element.16.meta_ref), custom_call_target="tpu_custom_call" | custom-call | tf_op jit(solution)/shard_map/forward/pallas_call | solution.py:388
  25.3 10.2 %grade.1 = (f32[64,512]{1,0:T(8,128)}, f32[8,128]{1,0:T(8,128)}) custom-call(f32[16,128]{1,0:T(8,128)} %get-tuple-element.18.score_ref, f32[16,1024]{1,0:T(8,128)} %get-tuple-element.19.hits_ref, f32[16,1024]{1,0:T(8,128)} %get-tuple-element.20.mass_ref, f32[8,8,128]{2,1,0:T(8,128)} %get-tuple-element.16.meta_ref), custom_call_target="tpu_custom_call" | custom-call | tf_op jit(solution)/shard_map/grade/pallas_call | solution.py:414
  35.5 14.1 %backward.1 = (bf16[180,64,128]{2,1,0:T(8,128)(2,1)}, bf16[512,128]{1,0:T(8,128)(2,1)}) custom-call(s32[64]{0:T(128)} %bitcast.24, bf16[180,64,128]{2,1,0:T(8,128)(2,1)} %bitcast.17, bf16[512,128]{1,0:T(8,128)(2,1)} %bitcast.19, f32[64,512]{1,0:T(8,128)} %get-tuple-element.17.lse_ref, f32[64,512]{1,0:T(8,128)} %get-tuple-element.21.grad_ref), custom_call_target="tpu_custom_call" | custom-call | tf_op jit(solution)/shard_map/backward/pallas_call | solution.py:436
  49.7 8.8 %collect.1 = (f32[64,128]{1,0:T(8,128)}, f32[8,128]{1,0:T(8,128)}) custom-call(bf16[8,64,128]{2,1,0:T(8,128)(2,1)} %bitcast.20, f32[8,128]{1,0:T(8,128)} %get-tuple-element.23.loss_ref), custom_call_target="tpu_custom_call" | custom-call | tf_op jit(solution)/shard_map/collect/pallas_call | solution.py:455
  58.5 1.2 %slice.3 = f32[1,1]{1,0:T(1,128)} slice(f32[8,128]{1,0:T(8,128)} %get-tuple-element.24), slice={[0:1], [0:1]} | slice | bytes 8 | tf_op jit(solution)/shard_map/slice | solution.py:475
  59.7 1.4 %copy.13 = f32[2,1,32,128]{3,2,1,0:T(8,128)} copy(f32[2,1,32,128]{3,2,1,0:T(8,128)} %bitcast.21) | data formatting | bytes 65536

commit v3 on v2

--- a/solution.py
+++ b/solution.py
@@ -26,7 +26,10 @@
         pl.semaphore_signal(
             barrier, inc=1, device_id={"rep": lax.rem(mine + step, replicas)}, device_id_type=MESH
         )
-    pl.semaphore_wait(barrier, groups - 1 + replicas - 1)
+
+
+def greeted(groups, replicas):
+    pl.semaphore_wait(pltpu.get_barrier_semaphore(), groups - 1 + replicas - 1)
 
 
 def share_kernel(
@@ -34,6 +37,7 @@
     all_queries, all_meta, query_buf, meta_buf, send_sem, recv_sem,
 ):
     me = lax.axis_index("grp")
+    greet(groups, 1, me, 0)
     count, ways = cand_ref.shape
     table = map_ref[...].astype(jnp.float32)
     ids = lax.broadcasted_iota(jnp.int32, (ways, table.shape[1]), 1)
@@ -54,10 +58,13 @@
         row = jnp.sum(jnp.where(diagonal, row, 0.0), axis=0, keepdims=True)
         meta_buf[me, q : q + 1, :ways] = row
     meta_buf[me, count : 2 * count, :ways] = prob
-    meta_buf[me, 2 * count : 3 * count, :] = jnp.broadcast_to(weights_ref[...], (count, LANES))
+    for q in range(count):
+        meta_buf[me, 2 * count + q : 2 * count + q + 1, :] = jnp.broadcast_to(
+            weights_ref[:, q : q + 1], (1, LANES)
+        )
     meta_buf[me, 3 * count : 4 * count, :] = jnp.broadcast_to(entropy, (count, LANES))
     query_buf[me] = queries_ref[...]
-    greet(groups, 1, me, 0)
+    greeted(groups, 1)
     copies = []
     for step in range(1, groups):
         peer = lax.rem(me + step, groups)
@@ -170,6 +177,7 @@
 ):
     me = lax.axis_index("grp")
     mine = lax.axis_index("rep")
+    greet(groups, replicas, me, mine)
     total, slot = score_ref.shape
     count = total // groups
     for source in range(groups):
@@ -181,7 +189,7 @@
     weight_buf[mine] = jnp.broadcast_to(
         jnp.sum(query_weight[...], axis=0, keepdims=True), weight_buf.shape[1:]
     )
-    greet(groups, replicas, me, mine)
+    greeted(groups, replicas)
     copies = []
     for step in range(1, groups):
         copies.append(
@@ -302,8 +310,9 @@
 ):
     me = lax.axis_index("grp")
     mine = lax.axis_index("rep")
+    greet(groups, replicas, me, mine)
     loss_buf[mine] = loss_ref[...]
-    greet(groups, replicas, me, mine)
+    greeted(groups, replicas)
     copies = []
     for step in range(1, groups):
         peer = lax.rem(me + step, groups)
@@ -334,7 +343,7 @@
     for copy in copies:
         copy.wait()
     grad_ref[...] = jnp.sum(arrived[...].astype(jnp.float32), axis=0)
-    loss_out[...] = jnp.sum(loss_buf[...], axis=0)
+    loss_out[...] = jnp.sum(loss_buf[...], axis=0)[:1, :1]
 
 
 def on_device(queries, passages, lengths, cand_ids, owner_map, teacher, weights):
@@ -371,7 +380,7 @@
         cand_ids[:, 0],
         owner_map,
         teacher[:, 0],
-        weights,
+        jnp.transpose(weights),
     )
     flat_queries = all_queries.reshape(width, dim)
     flat_passages = jnp.transpose(passages[:, 0], (1, 0, 2))
@@ -457,7 +466,7 @@
         name="collect",
         out_shape=[
             jax.ShapeDtypeStruct((own_rows, dim), f32),
-            jax.ShapeDtypeStruct((8, LANES), f32),
+            jax.ShapeDtypeStruct((1, 1), f32),
         ],
         in_specs=[VMEM_SPEC] * 2,
         out_specs=[VMEM_SPEC] * 2,
@@ -472,7 +481,7 @@
         compiler_params=pltpu.CompilerParams(collective_id=2, has_side_effects=True),
     )(partial.reshape(groups, own_rows, dim), loss_part)
     return (
-        loss[0, 0],
+        loss.reshape(()),
         query_grad.reshape(count, 1, query_len, dim),
         jnp.transpose(passage_grad, (1, 0, 2))[:, None],
     )

time: 61.5 us -> 60.5 us (0.984)
  local copies, waits for them, and re-layouts: 3.86 us -> 1.38 us
  between operations: 0.66 us -> 2.47 us
    unnamed x2 -> x1, local copies, waits for them, and re-layouts: 2.67 us -> 1.38 us
    slice x1 -> x0, local copies, waits for them, and re-layouts: 1.19 us -> none  [on_device(): loss[0, 0]]
where the time goes in v3:
time: 60.5 us; the launch traced here: 60.1 us
  Pallas kernels  56.3 us (93%)
  between operations  2.47 us (4%)
  local copies, waits for them, and re-layouts  1.38 us (2%)
    pallas_call x1, Pallas kernels, on_device(): pl.pallas_call(backward_kernel, name='backward', grid_spec=pltpu.Prefetch...  14.1 us
    pallas_call x1, Pallas kernels, on_device(): pl.pallas_call(functools.partial(forward_kernel, count, ways, block), nam...  12 us
    pallas_call x1, Pallas kernels, on_device(): pl.pallas_call(functools.partial(share_kernel, groups, block), name='shar...  11.2 us
    pallas_call x1, Pallas kernels, on_device(): pl.pallas_call(functools.partial(grade_kernel, groups, replicas), name='g...  10.1 us
    pallas_call x1, Pallas kernels, on_device(): pl.pallas_call(functools.partial(collect_kernel, groups, replicas), name=...  8.87 us
    unnamed x1, local copies, waits for them, and re-layouts  1.38 us

profile of v3, /device:TPU:0, one launch (start us, length us, event | category | flops | bytes accessed | tf_op | source)
XLA Modules:
  0.0 60.1 jit_solution(2324693448389282421)
XLA Ops:
  0.6 11.2 %share.1 = (bf16[8,64,128]{2,1,0:T(8,128)(2,1)}, f32[8,8,128]{2,1,0:T(8,128)}) custom-call(bf16[64,128]{1,0:T(8,128)(2,1)} %bitcast.23, s32[2,64]{1,0:T(2,128)} %bitcast.26, s32[1,512]{1,0:T(1,128)} %map_ref.1, f32[2,64]{1,0:T(2,128)} %bitcast.27, f32[1,2]{1,0:T(1,128)} %bitcast.28), custom_call_target="tpu_custom_call" | custom-call | tf_op jit(solution)/shard_map/share/pallas_call | solution.py:362
  11.8 12.0 %forward.1 = (f32[64,512]{1,0:T(8,128)}, f32[16,128]{1,0:T(8,128)}, f32[16,1024]{1,0:T(8,128)}, f32[16,1024]{1,0:T(8,128)}) custom-call(s32[64]{0:T(128)} %bitcast.24, bf16[180,64,128]{2,1,0:T(8,128)(2,1)} %bitcast.17, bf16[512,128]{1,0:T(8,128)(2,1)} %bitcast.19, f32[8,8,128]{2,1,0:T(8,128)} %get-tuple-element.16.meta_ref), custom_call_target="tpu_custom_call" | custom-call | tf_op jit(solution)/shard_map/forward/pallas_call | solution.py:397
  23.8 10.1 %grade.1 = (f32[64,512]{1,0:T(8,128)}, f32[8,128]{1,0:T(8,128)}) custom-call(f32[16,128]{1,0:T(8,128)} %get-tuple-element.18.score_ref, f32[16,1024]{1,0:T(8,128)} %get-tuple-element.19.hits_ref, f32[16,1024]{1,0:T(8,128)} %get-tuple-element.20.mass_ref, f32[8,8,128]{2,1,0:T(8,128)} %get-tuple-element.16.meta_ref), custom_call_target="tpu_custom_call" | custom-call | tf_op jit(solution)/shard_map/grade/pallas_call | solution.py:423
  33.9 14.1 %backward.1 = (bf16[180,64,128]{2,1,0:T(8,128)(2,1)}, bf16[512,128]{1,0:T(8,128)(2,1)}) custom-call(s32[64]{0:T(128)} %bitcast.25, bf16[180,64,128]{2,1,0:T(8,128)(2,1)} %bitcast.18, bf16[512,128]{1,0:T(8,128)(2,1)} %bitcast.20, f32[64,512]{1,0:T(8,128)} %get-tuple-element.17.lse_ref, f32[64,512]{1,0:T(8,128)} %get-tuple-element.21.grad_ref), custom_call_target="tpu_custom_call" | custom-call | tf_op jit(solution)/shard_map/backward/pallas_call | solution.py:445
  48.1 8.9 %collect.1 = (f32[64,128]{1,0:T(8,128)}, f32[1,1]{1,0:T(1,128)}) custom-call(bf16[8,64,128]{2,1,0:T(8,128)(2,1)} %bitcast.21, f32[8,128]{1,0:T(8,128)} %get-tuple-element.23.loss_ref), custom_call_target="tpu_custom_call" | custom-call | tf_op jit(solution)/shard_map/collect/pallas_call | solution.py:464
  57.6 1.4 %copy.14 = f32[2,1,32,128]{3,2,1,0:T(8,128)} copy(f32[2,1,32,128]{3,2,1,0:T(8,128)} %bitcast.22) | data formatting | bytes 65536
